TPU v7x, 32 devices: a whole 2x2x4 slice. The times are simulated.
32 devices in a mesh: clips: 2 (over x), tm: 4 (over y, core), height: 4 (over z).
Axes of the slice: x: 2, y: 2, z: 4, core: 2. Of those that a mesh axis runs over, the one named last changes fastest.
Arguments:
- features: bfloat16 [16, 16, 96, 512], P(('clips', 'tm'), 'height'), parts along dimension 0, may hold values from -1000 to 1000
- gain: float32 [512], replicated, may hold values from 0.1 to 1.9
- shift: float32 [512], replicated, may hold values from -3 to 3
- kernel: bfloat16 [3, 3, 3, 512, 256], replicated, may hold values from -0.0546875 to 0.0546875
- bias: float32 [256], replicated, may hold values from -3 to 3
Outputs:
- decoded: bfloat16 [16, 16, 96, 256], P(('clips', 'tm'), 'height'), parts along dimension 0
There are 2 independent parts, one for each index of `clips`. A program takes and returns all parts, laid end to end along the dimension named above; an argument that names none is the same for every part. Nothing has to cross between parts.
All inputs are finite; a program needn't handle non-finite values.
Results may differ from a plain program's by a relative error of at most 0.0055.
Values may be sent and summed in bfloat16 or wider, within the bound.
A program may use at most 64 MiB of HBM per device.

v0:
```python
import jax
import jax.numpy as jnp
from jax import lax
from jax.sharding import PartitionSpec as P

GROUPS = 32


epsilon = 1e-06


def passed_along(value, axis, steps):
    count = lax.axis_size(axis)
    initial, last = (max(0, -steps), min(count, count - steps))
    return lax.ppermute(value, axis, [(source, source + steps) for source in range(initial, last)])


def padded(block, sides, width):
    for axis, dim in sides:
        count = lax.axis_size(axis)
        forward = [(i, i + 1) for i in range(count - 1)]
        backward = [(target, source) for source, target in forward]
        low = lax.ppermute(
            lax.slice_in_dim(block, block.shape[dim] - width, None, axis=dim), axis, forward
        )
        high = lax.ppermute(lax.slice_in_dim(block, 0, width, axis=dim), axis, backward)
        block = jnp.concatenate([low, block, high], axis=dim)
    return block


def spatial(frames, kernel_plane):
    count_frames, padded_rows, padded_cols, channels = frames.shape
    inner_rows = padded_rows - 2
    inner_cols = padded_cols - 2
    summed = jnp.zeros(
        (count_frames * inner_rows * inner_cols, kernel_plane.shape[-1]), jnp.float32
    )
    for b in range(3):
        for c in range(3):
            window = frames[:, b : b + inner_rows, c : c + inner_cols, :].reshape(-1, channels)
            summed = summed + jnp.dot(
                window, kernel_plane[b, c], preferred_element_type=jnp.float32
            )
    return summed.reshape(count_frames, inner_rows, inner_cols, -1)


def pad_columns(frames):
    return jnp.pad(frames, ((0, 0), (0, 0), (1, 1), (0, 0)))


def on_device(features, gain, shift, kernel, bias):
    frames_dev, rows_dev, cols_dev, channels = features.shape
    per_group = channels // GROUPS
    wide_values = features.astype(jnp.float32).reshape(
        frames_dev, rows_dev, cols_dev, GROUPS, per_group
    )
    cells_total = (
        lax.axis_size("tm") * lax.axis_size("height") * frames_dev * rows_dev * cols_dev * per_group
    )
    local_sums = jnp.sum(wide_values, axis=(0, 1, 2, 4))
    squares = jnp.sum(wide_values * wide_values, axis=(0, 1, 2, 4))
    summed_all, squares_all = lax.psum((local_sums, squares), ("tm", "height"))
    group_mean = summed_all / cells_total
    group_var = squares_all / cells_total - group_mean * group_mean
    centered = wide_values - group_mean[:, None]
    normed = centered * lax.rsqrt(group_var + epsilon)[:, None]
    normed = normed.reshape(frames_dev, rows_dev, cols_dev, channels) * gain + shift
    activated = jax.nn.silu(normed).astype(jnp.bfloat16)
    tm_index = lax.axis_index("tm")
    first_pair = jnp.concatenate([activated[:1], activated[:1]], 0)
    earlier = passed_along(activated, "tm", 1)
    earlier = jnp.where(tm_index == 0, first_pair, earlier)
    slab = jnp.concatenate([earlier, activated], 0)
    slab = pad_columns(padded(slab, (("height", 1),), 1))
    output = jnp.zeros((frames_dev, rows_dev, cols_dev, kernel.shape[-1]), jnp.float32)
    for a in range(3):
        output = output + spatial(slab[a : a + frames_dev], kernel[a])
    return (output + bias).astype(jnp.bfloat16)


def solution(mesh):
    placed = (P(("clips", "tm"), "height", None, None), P(), P(), P(), P())
    return jax.shard_map(
        on_device,
        mesh=mesh,
        in_specs=placed,
        out_specs=P(("clips", "tm"), "height", None, None),
        check_vma=False,
    )
```

profile of v0, /device:TPU:4, one launch (start us, length us, event | category | flops | bytes accessed | tf_op | source)
XLA Modules:
  0.0 82.0 jit_solution(8100882752288773992)
XLA Ops:
  0.0 1.4 %convert_reduce_fusion = (f32[512]{0:T(512)S(1)}, f32[512]{0:T(512)S(1)}) fusion(bf16[2,4,96,512]{3,2,1,0:T(8,128)(2,1)} %param.5), kind=kLoop, calls=%fused_computation.10 | loop fusion | flops 1571840 | bytes 790528 | tf_op jit(solution)/shard_map/reduce_sum | solution.py:60
  1.4 0.1 reduce_sum.24
  1.5 0.1 reduce_sum.36
  1.5 0.1 reduce_sum.25
  1.7 0.1 reduce_sum.37
  1.8 32.7 %all-reduce.1 = (f32[32]{0:T(128)S(1)}, f32[32]{0:T(128)S(1)}) all-reduce(f32[32]{0:T(128)S(1)} %reduce_sum.37, f32[32]{0:T(128)S(1)} %reduce_sum.25), channel_id=1, replica_groups=mesh['clips'=2,'tm'=4,'height'=4] {'tm','height'}, use_global_device_ids=true, to_apply=%region_5.6 | all-reduce | flops 64 | bytes 512 | tf_op jit(solution)/shard_map/psum | solution.py:62
  34.5 0.1 mul.34
  34.5 0.1 mul.35
  34.6 0.1 sub.16
  34.7 0.1 sub.17
  34.8 1.7 %fusion.12 = bf16[2,4,96,512]{3,2,1,0:T(8,128)(2,1)S(1)} fusion(bf16[2,4,96,512]{3,2,1,0:T(8,128)(2,1)} %param.5, f32[512]{0:T(512)} %param.7, f32[512]{0:T(512)} %param.6, f32[512]{0:T(512)S(1)} %mul.35, f32[512]{0:T(512)S(1)} %sub.17), kind=kLoop, calls=%fused_computation.24 | loop fusion | flops 3932160 | bytes 1581056 | tf_op jit(solution)/shard_map/convert_element_type | solution.py:68
  36.5 1.9 %collective-permute-start = (bf16[2,4,96,512]{3,2,1,0:T(8,128)(2,1)S(1)}, bf16[2,4,96,512]{3,2,1,0:T(8,128)(2,1)S(1)}, u32[]{:S(2)}, u32[]{:S(2)}) collective-permute-start(bf16[2,4,96,512]{3,2,1,0:T(8,128)(2,1)S(1)} %fusion.12), channel_id=1, source_target_pairs={{0,4},{4,8},{8,12},{1,5},{5,9},{9,13},{2,6},{6,10},{10,14},{3,7},{... | collective-permute-start | bytes 2359304 | tf_op jit(solution)/shard_map/ppermute | solution.py:15
  38.5 3.8 %slice_bitcast_fusion.2 = (bf16[3,3,512,256]{3,2,1,0:T(8,128)(2,1)S(1)}, bf16[3,3,512,256]{3,2,1,0:T(8,128)(2,1)S(1)}, bf16[3,3,512,256]{3,2,1,0:T(8,128)(2,1)S(1)}) fusion(bf16[3,3,3,512,256]{4,3,2,1,0:T(8,128)(2,1)} %param.8), kind=kLoop, calls=%fused_computation.13 | loop fusion | bytes 14155776 | tf_op jit(solution)/shard_map/squeeze | solution.py:77
  42.3 0.4 fusion.24
  42.7 7.1 %collective-permute-done = bf16[2,4,96,512]{3,2,1,0:T(8,128)(2,1)S(1)} collective-permute-done((bf16[2,4,96,512]{3,2,1,0:T(8,128)(2,1)S(1)}, bf16[2,4,96,512]{3,2,1,0:T(8,128)(2,1)S(1)}, u32[]{:S(2)}, u32[]{:S(2)}) %collective-permute-start) | collective-permute-done | bytes 786464 | tf_op jit(solution)/shard_map/ppermute | solution.py:15
  49.8 0.1 maximum_select_fusion
  49.9 0.1 pad_maximum_fusion.3
  50.0 0.1 pad_maximum_fusion.1
  50.1 1.3 %collective-permute-start.1 = (bf16[4,1,96,512]{3,2,1,0:T(8,128)(2,1)S(1)}, bf16[4,1,96,512]{3,2,1,0:T(8,128)(2,1)S(1)}, u32[]{:S(2)}, u32[]{:S(2)}) collective-permute-start(bf16[4,1,96,512]{3,2,1,0:T(8,128)(2,1)S(1)} %get-tuple-element.38), channel_id=1, source_target_pairs={{0,1},{1,2},{2,3},{4,5},{5,6},{6,7},{8,9},{9,10},{10,11},{12,13},{... | collective-permute-start | bytes 1179656 | tf_op jit(solution)/shard_map/ppermute | solution.py:23
  51.4 1.5 %collective-permute-start.2 = (bf16[4,1,96,512]{3,2,1,0:T(8,128)(2,1)S(1)}, bf16[4,1,96,512]{3,2,1,0:T(8,128)(2,1)S(1)}, u32[]{:S(2)}, u32[]{:S(2)}) collective-permute-start(bf16[4,1,96,512]{3,2,1,0:T(8,128)(2,1)S(1)} %get-tuple-element.39), channel_id=1, source_target_pairs={{1,0},{2,1},{3,2},{5,4},{6,5},{7,6},{9,8},{10,9},{11,10},{13,12},{... | collective-permute-start | bytes 1179656 | tf_op jit(solution)/shard_map/ppermute | solution.py:26
  52.9 1.3 %fusion.32 = f32[768,256]{1,0:T(8,128)} fusion(bf16[768,512]{1,0:T(8,128)(2,1)S(1)} %bitcast.169, bf16[3,3,512,256]{3,2,1,0:T(8,128)(2,1)S(1)} %get-tuple-element.11), kind=kOutput, calls=%fused_computation.65 | convolution fusion | flops 201326592 | bytes 1835008 | tf_op jit(solution)/shard_map/dot_general | solution.py:41
  54.1 0.4 fusion.41
  54.5 2.1 %collective-permute-done.1 = bf16[4,1,96,512]{3,2,1,0:T(8,128)(2,1)S(1)} collective-permute-done((bf16[4,1,96,512]{3,2,1,0:T(8,128)(2,1)S(1)}, bf16[4,1,96,512]{3,2,1,0:T(8,128)(2,1)S(1)}, u32[]{:S(2)}, u32[]{:S(2)}) %collective-permute-start.1) | collective-permute-done | bytes 393248 | tf_op jit(solution)/shard_map/ppermute | solution.py:23
  56.6 4.4 %collective-permute-done.2 = bf16[4,1,96,512]{3,2,1,0:T(8,128)(2,1)S(1)} collective-permute-done((bf16[4,1,96,512]{3,2,1,0:T(8,128)(2,1)S(1)}, bf16[4,1,96,512]{3,2,1,0:T(8,128)(2,1)S(1)}, u32[]{:S(2)}, u32[]{:S(2)}) %collective-permute-start.2) | collective-permute-done | bytes 393248 | tf_op jit(solution)/shard_map/ppermute | solution.py:26
  61.1 0.5 maximum_maximum_fusion
  61.5 1.5 %fusion.47 = (bf16[2,4,96,512]{3,2,1,0:T(8,128)(2,1)}, bf16[2,4,96,512]{3,2,1,0:T(8,128)(2,1)}, bf16[2,4,96,512]{3,2,1,0:T(8,128)(2,1)S(1)}, bf16[2,4,96,512]{3,...) fusion(bf16[4,5,96,512]{3,2,1,0:T(8,128)(2,1)S(1)} %get-tuple-element.36, ...), kind=kLoop, calls=%fused_computation.95 | loop fusion | bytes 9437184 | tf_op jit(solution)/shard_map/slice | solution.py:40
  63.1 1.3 %fusion.30 = f32[768,256]{1,0:T(8,128)} fusion(bf16[768,512]{1,0:T(8,128)(2,1)S(1)} %bitcast.168, bf16[3,3,512,256]{3,2,1,0:T(8,128)(2,1)S(1)} %get-tuple-element.11), kind=kOutput, calls=%fused_computation.60 | convolution fusion | flops 201326592 | bytes 1835008 | tf_op jit(solution)/shard_map/dot_general | solution.py:41
  64.3 1.3 %fusion.35 = f32[768,256]{1,0:T(8,128)} fusion(bf16[768,512]{1,0:T(8,128)(2,1)S(1)} %bitcast.167, bf16[3,3,512,256]{3,2,1,0:T(8,128)(2,1)S(1)} %get-tuple-element.11), kind=kOutput, calls=%fused_computation.71 | convolution fusion | flops 201326592 | bytes 1835008 | tf_op jit(solution)/shard_map/dot_general | solution.py:41
  65.6 1.5 %select_maximum_fusion = bf16[4,6,98,512]{3,2,1,0:T(8,128)(2,1)S(1)} fusion(bf16[4,1,96,512]{3,2,1,0:T(8,128)(2,1)S(1)} %collective-permute-done.2, bf16[4,1,96,512]{3,2,1,0:T(8,128)(2,1)S(1)} %collective-permute-done.1, bf16[2,4,96,512]{3,2,1,0:T(8,128)(2,1)S(1)} %fusion.12, bf16[2,4,96,512]{3,2,1,0:T(8,128)(2,1)S(1)} %maximum_select_fusion), kind=kLoop, calls=%fused_computation.3 | loop fusion | flops 18063360 | bytes 4767744 | tf_op jit(solution)/shard_map/concatenate | solution.py:27
  67.1 4.6 %fusion.46 = (bf16[2,4,96,512]{3,2,1,0:T(8,128)(2,1)S(1)}, bf16[2,4,96,512]{3,2,1,0:T(8,128)(2,1)S(1)}, bf16[2,4,96,512]{3,2,1,0:T(8,128)(2,1)S(1)}, bf16[2,4,96...) fusion(bf16[4,6,98,512]{3,2,1,0:T(8,128)(2,1)S(1)} %select_maxi, ...), kind=kLoop, calls=%fused_computation.94 | loop fusion | bytes 28311552 | tf_op jit(solution)/shard_map/slice | solution.py:40
  71.7 0.4 fusion.29
  72.1 0.4 fusion.31
  72.5 0.0 copy-start.2
  72.5 0.4 fusion.33
  72.9 0.0 copy-start.1
  72.9 0.4 fusion.34
  73.2 0.0 copy-start
  73.2 0.4 fusion.36
  73.6 0.0 copy-done.2
  73.6 0.4 fusion.38
  74.0 0.1 copy-done.1
  74.1 0.4 fusion.44
  74.4 0.1 copy-done
  74.5 0.4 fusion.27
  74.9 0.4 fusion.22
  75.2 0.4 fusion.21
  75.6 0.4 fusion.23
  76.0 0.4 fusion.25
  76.3 0.4 fusion.26
  76.7 0.4 fusion.28
  77.1 0.4 fusion.37
  77.5 0.4 fusion.39
  77.8 0.4 fusion.40
  78.2 0.0 copy-start.3
  78.2 0.0 copy-start.4
  78.2 0.4 fusion.42
  78.6 0.4 fusion.43
  79.0 0.4 fusion.45
  79.3 0.2 copy-done.4
  79.6 0.2 copy-done.5
  79.8 0.4 fusion.20
  80.3 0.0 copy-start.6
  80.3 0.9 %fusion.17 = f32[768,256]{1,0:T(8,128)S(1)} fusion(f32[768,256]{1,0:T(8,128)S(1)} %fusion.21, f32[768,256]{1,0:T(8,128)S(1)} %fusion.22, f32[768,256]{1,0:T(8,128)S(1)} %fusion.23, bf16[768,512]{1,0:T(8,128)(2,1)S(1)} %bitcast.144, f32[768,256]{1,0:T(8,128)S(1)} %fusion.24, f32[768,256]{1,0:T(8,128)S(1)} %fusion.25, f32[768,256]{1,0:T(8,128)S(1)} %fusion.26, ...), kind=kOutput, calls=%fused_computation.30 | convolution fusion | flops 204865536 | bytes 15990784 | tf_op jit(solution)/shard_map/dot_general | solution.py:41
  81.2 0.8 add_convert_fusion
  (5 shorter events, 0.0 us)
Async XLA Ops:
  36.5 13.3 %collective-permute-start = (bf16[2,4,96,512]{3,2,1,0:T(8,128)(2,1)S(1)}, bf16[2,4,96,512]{3,2,1,0:T(8,128)(2,1)S(1)}, u32[]{:S(2)}, u32[]{:S(2)}) collective-permute-start(bf16[2,4,96,512]{3,2,1,0:T(8,128)(2,1)S(1)} %fusion.12), channel_id=1, source_target_pairs={{0,4},{4,8},{8,12},{1,5},{5,9},{9,13},{2,6},{6,10},{10,14},{3,7},{... | collective-permute-start | bytes 2359304 | tf_op jit(solution)/shard_map/ppermute | solution.py:15
  50.1 6.6 %collective-permute-start.1 = (bf16[4,1,96,512]{3,2,1,0:T(8,128)(2,1)S(1)}, bf16[4,1,96,512]{3,2,1,0:T(8,128)(2,1)S(1)}, u32[]{:S(2)}, u32[]{:S(2)}) collective-permute-start(bf16[4,1,96,512]{3,2,1,0:T(8,128)(2,1)S(1)} %get-tuple-element.38), channel_id=1, source_target_pairs={{0,1},{1,2},{2,3},{4,5},{5,6},{6,7},{8,9},{9,10},{10,11},{12,13},{... | collective-permute-start | bytes 1179656 | tf_op jit(solution)/shard_map/ppermute | solution.py:23
  51.4 9.7 %collective-permute-start.2 = (bf16[4,1,96,512]{3,2,1,0:T(8,128)(2,1)S(1)}, bf16[4,1,96,512]{3,2,1,0:T(8,128)(2,1)S(1)}, u32[]{:S(2)}, u32[]{:S(2)}) collective-permute-start(bf16[4,1,96,512]{3,2,1,0:T(8,128)(2,1)S(1)} %get-tuple-element.39), channel_id=1, source_target_pairs={{1,0},{2,1},{3,2},{5,4},{6,5},{7,6},{9,8},{10,9},{11,10},{13,12},{... | collective-permute-start | bytes 1179656 | tf_op jit(solution)/shard_map/ppermute | solution.py:26
  72.5 1.1 %copy-start.2 = (bf16[2,4,96,512]{3,2,1,0:T(8,128)(2,1)S(1)}, bf16[2,4,96,512]{3,2,1,0:T(8,128)(2,1)}, u32[]{:S(2)}) copy-start(bf16[2,4,96,512]{3,2,1,0:T(8,128)(2,1)} %get-tuple-element.44) | copy-start | bytes 2359300
  72.9 1.2 %copy-start.1 = (bf16[2,4,96,512]{3,2,1,0:T(8,128)(2,1)S(1)}, bf16[2,4,96,512]{3,2,1,0:T(8,128)(2,1)}, u32[]{:S(2)}) copy-start(bf16[2,4,96,512]{3,2,1,0:T(8,128)(2,1)} %get-tuple-element.30) | copy-start | bytes 2359300
  73.2 1.3 %copy-start = (bf16[2,4,96,512]{3,2,1,0:T(8,128)(2,1)S(1)}, bf16[2,4,96,512]{3,2,1,0:T(8,128)(2,1)}, u32[]{:S(2)}) copy-start(bf16[2,4,96,512]{3,2,1,0:T(8,128)(2,1)} %get-tuple-element.31) | copy-start | bytes 2359300
  78.2 1.1 %copy-start.3 = (f32[768,256]{1,0:T(8,128)S(1)}, f32[768,256]{1,0:T(8,128)}, u32[]{:S(2)}) copy-start(f32[768,256]{1,0:T(8,128)} %fusion.32) | copy-start | bytes 2359300
  78.2 1.4 %copy-start.4 = (f32[768,256]{1,0:T(8,128)S(1)}, f32[768,256]{1,0:T(8,128)}, u32[]{:S(2)}) copy-start(f32[768,256]{1,0:T(8,128)} %fusion.30) | copy-start | bytes 2359300
  78.2 1.6 %copy-start.5 = (f32[768,256]{1,0:T(8,128)S(1)}, f32[768,256]{1,0:T(8,128)}, u32[]{:S(2)}) copy-start(f32[768,256]{1,0:T(8,128)} %fusion.35) | copy-start | bytes 2359300
  80.3 0.9 %copy-start.6 = (f32[256]{0:T(256)S(1)}, f32[256]{0:T(256)}, u32[]{:S(2)}) copy-start(f32[256]{0:T(256)} %param.9) | copy-start | bytes 3076
where the time goes:
time: 82.3 us; the launch traced here: 82 us
  blocking collectives  32.7 us (40%)
  waiting for transfers between devices  13.7 us (17%)
  matrix products  13.1 us (16%)
  local copies, waits for them, and re-layouts  11.1 us (13%)
  other arithmetic  6.37 us (8%)
  starting transfers between devices  4.71 us (6%)
    psum x1, blocking collectives, on_device(): summed_all, squares_all = lax.psum((local_sums, squares), ('tm', 'height'))  32.7 us
    dot_general x27, matrix products, spatial(): jnp.dot(window, kernel_plane[b, c], preferred_element_type=jnp.float32)  13.1 us
    ppermute x1, waiting for transfers between devices, passed_along(): lax.ppermute(value, axis, [(source, source + steps) for source in range(i...  7.11 us
    slice x2, local copies, waits for them, and re-layouts, spatial(): frames[:, b:b + inner_rows, c:c + inner_cols, :].reshape(-1, channels)  6.15 us
    ppermute x1, waiting for transfers between devices, padded(): lax.ppermute(lax.slice_in_dim(block, 0, width, axis=dim), axis, backward)  4.42 us
    squeeze x1, local copies, waits for them, and re-layouts, on_device(): output = output + spatial(slab[a:a + frames_dev], kernel[a])  3.84 us
    ppermute x1, waiting for transfers between devices, padded(): lax.ppermute(lax.slice_in_dim(block, block.shape[dim] - width, None, axis...  2.14 us
    concatenate x2, other arithmetic, padded(): block = jnp.concatenate([low, block, high], axis=dim)  1.97 us
  transfers between devices with their start and end apart: 3, of which 3 were waited for; matrix products, arithmetic and copies ran while one was open for 7% of the time, Pallas kernels for 0%

commit v1 on v0

v1 whole, which is shorter than its diff:
```python
import functools

import jax
import jax.numpy as jnp
from jax import lax
from jax.experimental import pallas as pl
from jax.experimental.pallas import tpu as pltpu
from jax.sharding import PartitionSpec as P

GROUPS = 32
EPSILON = 1e-06
MESH = pl.DeviceIdType.MESH
F32 = jnp.float32
BF16 = jnp.bfloat16


def group_sums(values, per_group):
    lanes = values.shape[-1]
    lane = lax.broadcasted_iota(jnp.int32, values.shape, values.ndim - 1)
    step = 1
    while step < per_group:
        up = pltpu.roll(values, lanes - step, values.ndim - 1)
        down = pltpu.roll(values, step, values.ndim - 1)
        values = values + jnp.where((lane & step) == 0, up, down)
        step *= 2
    return values


def body(
    n_tm,
    n_h,
    x_hbm,
    gain_ref,
    shift_ref,
    w_hbm,
    bias_ref,
    out_ref,
    x_vm,
    w_vm,
    top_vm,
    bot_vm,
    st1,
    st2,
    lhs,
    prod,
    nbuf,
    rbuf,
    x_sem,
    w_sem,
    s1_send,
    s1_recv,
    s2_send,
    s2_recv,
    h_send,
    h_recv,
    n_send,
    n_recv,
):
    frames, rows, cols, channels = x_vm.shape
    per_group = channels // GROUPS
    tm = lax.axis_index("tm")
    hh = lax.axis_index("height")

    barrier = pltpu.get_barrier_semaphore()
    for d in range(1, n_h):
        pl.semaphore_signal(
            barrier, inc=1, device_id={"height": lax.rem(hh + d, n_h)}, device_id_type=MESH
        )
    for d in range(1, n_tm):
        pl.semaphore_signal(
            barrier, inc=1, device_id={"tm": lax.rem(tm + d, n_tm)}, device_id_type=MESH
        )
    x_copy = pltpu.make_async_copy(x_hbm, x_vm, x_sem)
    x_copy.start()
    w_copies = [
        [pltpu.make_async_copy(w_hbm.at[a, :, c], w_vm.at[a, c], w_sem.at[a, c]) for c in range(3)]
        for a in range(3)
    ]
    for a in range(3):
        for c in range(3):
            w_copies[a][c].start()

    x_copy.wait()
    sums = jnp.zeros((8, channels), F32)
    squares = jnp.zeros((8, channels), F32)
    for f in range(frames):
        for r in range(rows):
            v = x_vm[f, r].astype(F32).reshape(cols // 8, 8, channels)
            sums = sums + jnp.sum(v, axis=0)
            squares = squares + jnp.sum(v * v, axis=0)
    st1[0, 0:1] = jnp.sum(sums, axis=0, keepdims=True)
    st1[0, 1:2] = jnp.sum(squares, axis=0, keepdims=True)

    pl.semaphore_wait(barrier, n_h + n_tm - 2)

    def stage(buf, send, recv, axis, me, count):
        copies = []
        for d in range(1, count):
            copies.append(
                pltpu.make_async_remote_copy(
                    src_ref=buf.at[0],
                    dst_ref=buf.at[d],
                    send_sem=send.at[d],
                    recv_sem=recv.at[d],
                    device_id={axis: lax.rem(me + d, count)},
                    device_id_type=MESH,
                )
            )
        return copies

    stage1 = stage(st1, s1_send, s1_recv, "tm", tm, n_tm)
    stage2 = stage(st2, s2_send, s2_recv, "height", hh, n_h)
    for copy in stage1:
        copy.start()
    to_next = pltpu.make_async_remote_copy(
        src_ref=x_hbm.at[:, rows - 1],
        dst_ref=top_vm,
        send_sem=h_send.at[0],
        recv_sem=h_recv.at[0],
        device_id={"height": lax.rem(hh + 1, n_h)},
        device_id_type=MESH,
    )
    to_last = pltpu.make_async_remote_copy(
        src_ref=x_hbm.at[:, 0],
        dst_ref=bot_vm,
        send_sem=h_send.at[1],
        recv_sem=h_recv.at[1],
        device_id={"height": lax.rem(hh + n_h - 1, n_h)},
        device_id_type=MESH,
    )
    total = st1[0]
    for d in range(1, n_tm):
        stage1[d - 1].wait_recv()
        total = total + st1[d]
    st2[0] = total
    for copy in stage2:
        copy.start()

    @pl.when(hh < n_h - 1)
    def _():
        to_next.start()

    @pl.when(hh > 0)
    def _():
        to_last.start()

    for d in range(1, n_h):
        stage2[d - 1].wait_recv()
        total = total + st2[d]
    cells = n_tm * n_h * frames * rows * cols * per_group
    means = group_sums(total, per_group) / cells
    mean = means[0:1]
    var = jnp.maximum(means[1:2] - mean * mean, 0.0)
    scale = gain_ref[...] * lax.rsqrt(var + EPSILON)
    half_offset = 0.5 * (shift_ref[...] - mean * scale)
    half_scale = 0.5 * scale

    def activate(v):
        h = v.astype(F32) * half_scale + half_offset
        return (h + h * jnp.tanh(h)).astype(BF16)

    row_sets = (tuple(range(1, rows - 1)), (0, rows - 1))
    per_set = 2 * cols

    def place(row, f, value):
        for s in range(2):
            for q, i in enumerate(row_sets[s]):
                b = row - i + 1
                if 0 <= b <= 2:
                    lhs[
                        s,
                        f * per_set + q * cols : f * per_set + (q + 1) * cols,
                        b * channels : (b + 1) * channels,
                    ] = value

    for f in range(frames):
        for r in range(rows):
            place(r, f, activate(x_vm[f, r]))

    m = frames * per_set
    position = lax.rem(lax.broadcasted_iota(jnp.int32, (m, 1), 0), cols)
    not_first = position != 0
    not_last = position != cols - 1

    def product(a, s):
        def tap(c):
            weights = w_vm[a, c].reshape(3 * channels, w_vm.shape[-1])
            return jnp.dot(lhs[s], weights, preferred_element_type=F32)

        low = jnp.where(not_first, pltpu.roll(tap(0), 1, 0), 0.0)
        high = jnp.where(not_last, pltpu.roll(tap(2), m - 1, 0), 0.0)
        prod[a, s] = low + tap(1) + high

    def sends(s, k):
        return pltpu.make_async_remote_copy(
            src_ref=nbuf.at[s, k],
            dst_ref=rbuf.at[s, k],
            send_sem=n_send.at[s, k],
            recv_sem=n_recv.at[s, k],
            device_id={"tm": lax.rem(tm + 1, n_tm)},
            device_id_type=MESH,
        )

    def send(s, k):
        @pl.when(tm < n_tm - 1)
        def _():
            sends(s, k).start()

    def wait_weights(a):
        for c in range(3):
            w_copies[a][c].wait()

    def early(s):
        if s == 0:
            wait_weights(0)
        product(0, s)
        nbuf[s, 1] = prod[0, s, per_set:].astype(BF16)
        send(s, 1)
        if s == 0:
            wait_weights(1)
        product(1, s)
        nbuf[s, 0] = (prod[0, s, :per_set] + prod[1, s, per_set:]).astype(BF16)
        send(s, 0)

        @pl.when(tm == 0)
        def _():
            rbuf[s, 0] = (prod[0, s, :per_set] + prod[1, s, :per_set]).astype(BF16)
            rbuf[s, 1] = prod[0, s, :per_set].astype(BF16)

    early(0)

    @pl.when(hh > 0)
    def _():
        to_next.wait_recv()
        for f in range(frames):
            place(-1, f, activate(top_vm[f]))

    @pl.when(hh == 0)
    def _():
        for f in range(frames):
            place(-1, f, jnp.zeros((cols, channels), BF16))

    @pl.when(hh < n_h - 1)
    def _():
        to_last.wait_recv()
        for f in range(frames):
            place(rows, f, activate(bot_vm[f]))

    @pl.when(hh == n_h - 1)
    def _():
        for f in range(frames):
            place(rows, f, jnp.zeros((cols, channels), BF16))

    early(1)
    wait_weights(2)
    product(2, 0)
    product(2, 1)

    bias = bias_ref[...]
    for s in range(2):
        for k in (1, 0):

            @pl.when(tm > 0)
            def _():
                sends(s, k).wait_recv()

            own = prod[2, s, k * per_set : (k + 1) * per_set]
            if k == 1:
                own = own + prod[1, s, :per_set]
            value = (own + rbuf[s, k].astype(F32) + bias).astype(BF16)
            for q, i in enumerate(row_sets[s]):
                out_ref[k, i] = value[q * cols : (q + 1) * cols]

    for copy in stage1 + stage2:
        copy.wait_send()

    @pl.when(hh < n_h - 1)
    def _():
        to_next.wait_send()

    @pl.when(hh > 0)
    def _():
        to_last.wait_send()

    @pl.when(tm < n_tm - 1)
    def _():
        for s in range(2):
            for k in range(2):
                sends(s, k).wait_send()


def solution(mesh):
    n_tm, n_h = mesh.shape["tm"], mesh.shape["height"]

    def on_device(features, gain, shift, kernel, bias):
        frames, rows, cols, channels = features.shape
        c_out = kernel.shape[-1]
        assert frames == 2 and rows == 4
        per_set = 2 * cols
        vmem = pl.BlockSpec(memory_space=pltpu.VMEM)
        anywhere = pl.BlockSpec(memory_space=pl.ANY)
        dma = pltpu.SemaphoreType.DMA
        return pl.pallas_call(
            functools.partial(body, n_tm, n_h),
            out_shape=jax.ShapeDtypeStruct((frames, rows, cols, c_out), BF16),
            in_specs=[anywhere, vmem, vmem, anywhere, vmem],
            out_specs=vmem,
            scratch_shapes=[
                pltpu.VMEM((frames, rows, cols, channels), BF16),
                pltpu.VMEM((3, 3, 3, channels, c_out), BF16),
                pltpu.VMEM((frames, cols, channels), BF16),
                pltpu.VMEM((frames, cols, channels), BF16),
                pltpu.VMEM((n_tm, 2, channels), F32),
                pltpu.VMEM((n_h, 2, channels), F32),
                pltpu.VMEM((2, frames * per_set, 3 * channels), BF16),
                pltpu.VMEM((3, 2, frames * per_set, c_out), F32),
                pltpu.VMEM((2, 2, per_set, c_out), BF16),
                pltpu.VMEM((2, 2, per_set, c_out), BF16),
                dma,
                dma((3, 3)),
                dma((n_tm,)),
                dma((n_tm,)),
                dma((n_h,)),
                dma((n_h,)),
                dma((2,)),
                dma((2,)),
                dma((2, 2)),
                dma((2, 2)),
            ],
            compiler_params=pltpu.CompilerParams(collective_id=0, has_side_effects=True),
        )(features, gain.reshape(1, -1), shift.reshape(1, -1), kernel, bias.reshape(1, -1))

    placed = (P(("clips", "tm"), "height", None, None), P(), P(), P(), P())
    return jax.shard_map(
        on_device,
        mesh=mesh,
        in_specs=placed,
        out_specs=P(("clips", "tm"), "height", None, None),
        check_vma=False,
    )
```

time: 82.3 us -> 25.3 us (0.31)
  the two profiles are of different devices: /device:TPU:4 before, /device:TPU:0 now
where the time goes in v1:
time: 25.3 us; the launch traced here: 25.1 us
  Pallas kernels  23.3 us (92%)
  local copies, waits for them, and re-layouts  1.77 us (7%)
    pallas_call x1, Pallas kernels, on_device(): pl.pallas_call(functools.partial(body, n_tm, n_h), out_shape=jax.ShapeDty...  23.3 us
    unnamed x1, local copies, waits for them, and re-layouts  1.77 us

profile of v1, /device:TPU:0, one launch (start us, length us, event | category | flops | bytes accessed | tf_op | source)
XLA Modules:
  0.0 25.1 jit_solution(10916144208095604737)
XLA Ops:
  0.0 23.3 %shard_map.55 = bf16[2,4,96,256]{3,2,1,0:T(8,128)(2,1)} custom-call(bf16[2,4,96,512]{3,2,1,0:T(8,128)(2,1)} %x_hbm.1, f32[1,512]{1,0:T(1,128)} %bitcast.3, f32[1,512]{1,0:T(1,128)} %bitcast.4, bf16[3,3,3,512,256]{4,3,2,1,0:T(8,128)(2,1)} %w_hbm.1, f32[1,256]{1,0:T(1,128)} %bitcast.5), custom_call_target="tpu_custom_call" | custom-call | tf_op jit(solution)/shard_map/pallas_call | solution.py:303
  23.3 1.8 %copy.7 = bf16[2,4,96,256]{3,2,1,0:T(8,128)(2,1)} copy(bf16[2,4,96,256]{3,2,1,0:T(8,128)(2,1)} %shard_map.55) | data formatting | bytes 786432

commit v2 on v1

--- a/solution.py
+++ b/solution.py
@@ -30,27 +30,28 @@
     n_tm,
     n_h,
     x_hbm,
+    gain_hbm,
+    shift_hbm,
+    w_hbm,
+    bias_hbm,
+    out_ref,
+    x_vm,
     gain_ref,
     shift_ref,
-    w_hbm,
     bias_ref,
-    out_ref,
-    x_vm,
     w_vm,
     top_vm,
     bot_vm,
-    st1,
-    st2,
+    stats,
     lhs,
     prod,
     nbuf,
     rbuf,
     x_sem,
+    p_sem,
     w_sem,
-    s1_send,
-    s1_recv,
-    s2_send,
-    s2_recv,
+    s_send,
+    s_recv,
     h_send,
     h_recv,
     n_send,
@@ -62,25 +63,29 @@
     hh = lax.axis_index("height")
 
     barrier = pltpu.get_barrier_semaphore()
-    for d in range(1, n_h):
-        pl.semaphore_signal(
-            barrier, inc=1, device_id={"height": lax.rem(hh + d, n_h)}, device_id_type=MESH
-        )
-    for d in range(1, n_tm):
-        pl.semaphore_signal(
-            barrier, inc=1, device_id={"tm": lax.rem(tm + d, n_tm)}, device_id_type=MESH
-        )
+    count = n_tm * n_h
+    me = tm * n_h + hh
+
+    def peer(d):
+        other = lax.rem(me + d, count)
+        return {"tm": lax.div(other, n_h), "height": lax.rem(other, n_h)}
+
+    for d in range(1, count):
+        pl.semaphore_signal(barrier, inc=1, device_id=peer(d), device_id_type=MESH)
     x_copy = pltpu.make_async_copy(x_hbm, x_vm, x_sem)
     x_copy.start()
+    small = ((gain_hbm, gain_ref), (shift_hbm, shift_ref), (bias_hbm, bias_ref))
+    p_copies = [pltpu.make_async_copy(*pair, p_sem.at[i]) for i, pair in enumerate(small)]
+    for copy in p_copies:
+        copy.start()
     w_copies = [
         [pltpu.make_async_copy(w_hbm.at[a, :, c], w_vm.at[a, c], w_sem.at[a, c]) for c in range(3)]
         for a in range(3)
     ]
+    x_copy.wait()
     for a in range(3):
         for c in range(3):
             w_copies[a][c].start()
-
-    x_copy.wait()
     sums = jnp.zeros((8, channels), F32)
     squares = jnp.zeros((8, channels), F32)
     for f in range(frames):
@@ -88,29 +93,23 @@
             v = x_vm[f, r].astype(F32).reshape(cols // 8, 8, channels)
             sums = sums + jnp.sum(v, axis=0)
             squares = squares + jnp.sum(v * v, axis=0)
-    st1[0, 0:1] = jnp.sum(sums, axis=0, keepdims=True)
-    st1[0, 1:2] = jnp.sum(squares, axis=0, keepdims=True)
-
-    pl.semaphore_wait(barrier, n_h + n_tm - 2)
-
-    def stage(buf, send, recv, axis, me, count):
-        copies = []
-        for d in range(1, count):
-            copies.append(
-                pltpu.make_async_remote_copy(
-                    src_ref=buf.at[0],
-                    dst_ref=buf.at[d],
-                    send_sem=send.at[d],
-                    recv_sem=recv.at[d],
-                    device_id={axis: lax.rem(me + d, count)},
-                    device_id_type=MESH,
-                )
-            )
-        return copies
-
-    stage1 = stage(st1, s1_send, s1_recv, "tm", tm, n_tm)
-    stage2 = stage(st2, s2_send, s2_recv, "height", hh, n_h)
-    for copy in stage1:
+    stats[0, 0:1] = jnp.sum(sums, axis=0, keepdims=True)
+    stats[0, 1:2] = jnp.sum(squares, axis=0, keepdims=True)
+
+    pl.semaphore_wait(barrier, count - 1)
+
+    shares = [
+        pltpu.make_async_remote_copy(
+            src_ref=stats.at[0],
+            dst_ref=stats.at[d],
+            send_sem=s_send.at[d],
+            recv_sem=s_recv.at[d],
+            device_id=peer(d),
+            device_id_type=MESH,
+        )
+        for d in range(1, count)
+    ]
+    for copy in shares:
         copy.start()
     to_next = pltpu.make_async_remote_copy(
         src_ref=x_hbm.at[:, rows - 1],
@@ -128,14 +127,6 @@
         device_id={"height": lax.rem(hh + n_h - 1, n_h)},
         device_id_type=MESH,
     )
-    total = st1[0]
-    for d in range(1, n_tm):
-        stage1[d - 1].wait_recv()
-        total = total + st1[d]
-    st2[0] = total
-    for copy in stage2:
-        copy.start()
-
     @pl.when(hh < n_h - 1)
     def _():
         to_next.start()
@@ -144,9 +135,11 @@
     def _():
         to_last.start()
 
-    for d in range(1, n_h):
-        stage2[d - 1].wait_recv()
-        total = total + st2[d]
+    for copy in shares:
+        copy.wait_recv()
+    total = jnp.sum(stats[...], axis=0)
+    for copy in p_copies:
+        copy.wait()
     cells = n_tm * n_h * frames * rows * cols * per_group
     means = group_sums(total, per_group) / cells
     mean = means[0:1]
@@ -201,11 +194,6 @@
             device_id_type=MESH,
         )
 
-    def send(s, k):
-        @pl.when(tm < n_tm - 1)
-        def _():
-            sends(s, k).start()
-
     def wait_weights(a):
         for c in range(3):
             w_copies[a][c].wait()
@@ -213,14 +201,16 @@
     def early(s):
         if s == 0:
             wait_weights(0)
+            wait_weights(1)
         product(0, s)
+        product(1, s)
         nbuf[s, 1] = prod[0, s, per_set:].astype(BF16)
-        send(s, 1)
-        if s == 0:
-            wait_weights(1)
-        product(1, s)
         nbuf[s, 0] = (prod[0, s, :per_set] + prod[1, s, per_set:]).astype(BF16)
-        send(s, 0)
+
+        @pl.when(tm < n_tm - 1)
+        def _():
+            sends(s, 1).start()
+            sends(s, 0).start()
 
         @pl.when(tm == 0)
         def _():
@@ -271,7 +261,7 @@
             for q, i in enumerate(row_sets[s]):
                 out_ref[k, i] = value[q * cols : (q + 1) * cols]
 
-    for copy in stage1 + stage2:
+    for copy in shares:
         copy.wait_send()
 
     @pl.when(hh < n_h - 1)
@@ -298,36 +288,39 @@
         assert frames == 2 and rows == 4
         per_set = 2 * cols
         vmem = pl.BlockSpec(memory_space=pltpu.VMEM)
-        anywhere = pl.BlockSpec(memory_space=pl.ANY)
+        hbm = pl.BlockSpec(memory_space=pltpu.HBM)
         dma = pltpu.SemaphoreType.DMA
         return pl.pallas_call(
             functools.partial(body, n_tm, n_h),
-            out_shape=jax.ShapeDtypeStruct((frames, rows, cols, c_out), BF16),
-            in_specs=[anywhere, vmem, vmem, anywhere, vmem],
+            out_shape=pltpu.VMEM((frames, rows, cols, c_out), BF16),
+            in_specs=[hbm] * 5,
             out_specs=vmem,
             scratch_shapes=[
                 pltpu.VMEM((frames, rows, cols, channels), BF16),
+                pltpu.VMEM((1, channels), F32),
+                pltpu.VMEM((1, channels), F32),
+                pltpu.VMEM((1, c_out), F32),
                 pltpu.VMEM((3, 3, 3, channels, c_out), BF16),
                 pltpu.VMEM((frames, cols, channels), BF16),
                 pltpu.VMEM((frames, cols, channels), BF16),
-                pltpu.VMEM((n_tm, 2, channels), F32),
-                pltpu.VMEM((n_h, 2, channels), F32),
+                pltpu.VMEM((n_tm * n_h, 2, channels), F32),
                 pltpu.VMEM((2, frames * per_set, 3 * channels), BF16),
                 pltpu.VMEM((3, 2, frames * per_set, c_out), F32),
                 pltpu.VMEM((2, 2, per_set, c_out), BF16),
                 pltpu.VMEM((2, 2, per_set, c_out), BF16),
                 dma,
+                dma((3,)),
                 dma((3, 3)),
-                dma((n_tm,)),
-                dma((n_tm,)),
-                dma((n_h,)),
-                dma((n_h,)),
+                dma((n_tm * n_h,)),
+                dma((n_tm * n_h,)),
                 dma((2,)),
                 dma((2,)),
                 dma((2, 2)),
                 dma((2, 2)),
             ],
-            compiler_params=pltpu.CompilerParams(collective_id=0, has_side_effects=True),
+            compiler_params=pltpu.CompilerParams(
+                collective_id=0, has_side_effects=True, vmem_limit_bytes=67_043_328 - 640 * 2**10
+            ),
         )(features, gain.reshape(1, -1), shift.reshape(1, -1), kernel, bias.reshape(1, -1))
 
     placed = (P(("clips", "tm"), "height", None, None), P(), P(), P(), P())

time: 25.3 us -> 18.5 us (0.73)
  Pallas kernels: 23.3 us -> 17.6 us
  local copies, waits for them, and re-layouts: 1.77 us -> 0.75 us
    pallas_call x1, Pallas kernels: 23.3 us -> 17.6 us  [on_device(): pl.pallas_call(functools.partial(body, n_tm, n_h), out_shape=pltpu.VMEM((...]
    unnamed x1, local copies, waits for them, and re-layouts: 1.77 us -> 0.75 us
where the time goes in v2:
time: 18.5 us; the launch traced here: 18.4 us
  Pallas kernels  17.6 us (95%)
  local copies, waits for them, and re-layouts  0.75 us (4%)
    pallas_call x1, Pallas kernels, on_device(): pl.pallas_call(functools.partial(body, n_tm, n_h), out_shape=pltpu.VMEM((...  17.6 us
    unnamed x1, local copies, waits for them, and re-layouts  0.75 us

profile of v2, /device:TPU:0, one launch (start us, length us, event | category | flops | bytes accessed | tf_op | source)
XLA Modules:
  0.0 18.4 jit_solution(5056827243870241710)
XLA Ops:
  0.0 17.6 %shard_map.55 = bf16[2,4,96,256]{3,2,1,0:T(8,128)(2,1)S(1)} custom-call(bf16[2,4,96,512]{3,2,1,0:T(8,128)(2,1)} %x_hbm.1, f32[1,512]{1,0:T(1,128)} %bitcast.3, f32[1,512]{1,0:T(1,128)} %bitcast.4, bf16[3,3,3,512,256]{4,3,2,1,0:T(8,128)(2,1)} %w_hbm.1, f32[1,256]{1,0:T(1,128)} %bitcast.5), custom_call_target="tpu_custom_call" | custom-call | tf_op jit(solution)/shard_map/pallas_call | solution.py:293
  17.6 0.7 %copy.7 = bf16[2,4,96,256]{3,2,1,0:T(8,128)(2,1)} copy(bf16[2,4,96,256]{3,2,1,0:T(8,128)(2,1)S(1)} %shard_map.55) | data formatting | bytes 786432

commit v3 on v2

--- a/solution.py
+++ b/solution.py
@@ -14,16 +14,25 @@
 BF16 = jnp.bfloat16
 
 
-def group_sums(values, per_group):
+LANES = 128
+
+
+def group_sums(values, group):
     lanes = values.shape[-1]
     lane = lax.broadcasted_iota(jnp.int32, values.shape, values.ndim - 1)
     step = 1
-    while step < per_group:
+    while step < group:
         up = pltpu.roll(values, lanes - step, values.ndim - 1)
         down = pltpu.roll(values, step, values.ndim - 1)
         values = values + jnp.where((lane & step) == 0, up, down)
         step *= 2
     return values
+
+
+def own_lanes(parts):
+    lane = lax.broadcasted_iota(jnp.int32, (parts, LANES), 1)
+    row = lax.broadcasted_iota(jnp.int32, (parts, LANES), 0)
+    return lax.rem(lane, parts) == row
 
 
 def body(
@@ -93,8 +102,16 @@
             v = x_vm[f, r].astype(F32).reshape(cols // 8, 8, channels)
             sums = sums + jnp.sum(v, axis=0)
             squares = squares + jnp.sum(v * v, axis=0)
-    stats[0, 0:1] = jnp.sum(sums, axis=0, keepdims=True)
-    stats[0, 1:2] = jnp.sum(squares, axis=0, keepdims=True)
+    blocks = channels // LANES
+    parts = 2 * blocks
+    assert parts <= per_group <= LANES
+    sums = jnp.sum(sums, axis=0, keepdims=True)
+    squares = jnp.sum(squares, axis=0, keepdims=True)
+    stacked = jnp.concatenate(
+        [v[:, k * LANES : (k + 1) * LANES] for v in (sums, squares) for k in range(blocks)], axis=0
+    )
+    spread = jnp.where(own_lanes(parts), group_sums(stacked, per_group), 0.0)
+    stats[0] = jnp.sum(spread, axis=0, keepdims=True)
 
     pl.semaphore_wait(barrier, count - 1)
 
@@ -141,12 +158,16 @@
     for copy in p_copies:
         copy.wait()
     cells = n_tm * n_h * frames * rows * cols * per_group
-    means = group_sums(total, per_group) / cells
-    mean = means[0:1]
-    var = jnp.maximum(means[1:2] - mean * mean, 0.0)
-    scale = gain_ref[...] * lax.rsqrt(var + EPSILON)
-    half_offset = 0.5 * (shift_ref[...] - mean * scale)
-    half_scale = 0.5 * scale
+    means = group_sums(jnp.where(own_lanes(parts), total, 0.0), parts) * (1.0 / cells)
+    mean = means[:blocks]
+    var = jnp.maximum(means[blocks:] - mean * mean, 0.0)
+    inverse = lax.rsqrt(var + EPSILON)
+
+    def one_row(v):
+        return jnp.concatenate([v[k : k + 1] for k in range(blocks)], axis=1)
+
+    half_scale = 0.5 * gain_ref[...] * one_row(inverse)
+    half_offset = 0.5 * shift_ref[...] - one_row(mean) * half_scale
 
     def activate(v):
         h = v.astype(F32) * half_scale + half_offset
@@ -176,13 +197,16 @@
     not_last = position != cols - 1
 
     def product(a, s):
-        def tap(c):
+        def tap(c, start, stop):
             weights = w_vm[a, c].reshape(3 * channels, w_vm.shape[-1])
-            return jnp.dot(lhs[s], weights, preferred_element_type=F32)
-
-        low = jnp.where(not_first, pltpu.roll(tap(0), 1, 0), 0.0)
-        high = jnp.where(not_last, pltpu.roll(tap(2), m - 1, 0), 0.0)
-        prod[a, s] = low + tap(1) + high
+            return jnp.dot(lhs[s, start:stop], weights, preferred_element_type=F32)
+
+        low = jnp.where(not_first, pltpu.roll(tap(0, 0, m), 1, 0), 0.0)
+        high = jnp.where(not_last, pltpu.roll(tap(2, 0, m), m - 1, 0), 0.0)
+        sides = low + high
+        for start in (0, per_set):
+            stop = start + per_set
+            prod[a, s, start:stop] = sides[start:stop] + tap(1, start, stop)
 
     def sends(s, k):
         return pltpu.make_async_remote_copy(
@@ -194,6 +218,11 @@
             device_id_type=MESH,
         )
 
+    def send(s, k):
+        @pl.when(tm < n_tm - 1)
+        def _():
+            sends(s, k).start()
+
     def wait_weights(a):
         for c in range(3):
             w_copies[a][c].wait()
@@ -203,19 +232,11 @@
             wait_weights(0)
             wait_weights(1)
         product(0, s)
+        nbuf[s, 1] = prod[0, s, per_set:].astype(BF16)
+        send(s, 1)
         product(1, s)
-        nbuf[s, 1] = prod[0, s, per_set:].astype(BF16)
         nbuf[s, 0] = (prod[0, s, :per_set] + prod[1, s, per_set:]).astype(BF16)
-
-        @pl.when(tm < n_tm - 1)
-        def _():
-            sends(s, 1).start()
-            sends(s, 0).start()
-
-        @pl.when(tm == 0)
-        def _():
-            rbuf[s, 0] = (prod[0, s, :per_set] + prod[1, s, :per_set]).astype(BF16)
-            rbuf[s, 1] = prod[0, s, :per_set].astype(BF16)
+        send(s, 0)
 
     early(0)
 
@@ -241,8 +262,8 @@
         for f in range(frames):
             place(rows, f, jnp.zeros((cols, channels), BF16))
 
+    wait_weights(2)
     early(1)
-    wait_weights(2)
     product(2, 0)
     product(2, 1)
 
@@ -255,9 +276,14 @@
                 sends(s, k).wait_recv()
 
             own = prod[2, s, k * per_set : (k + 1) * per_set]
+            first = prod[0, s, :per_set]
+            other = prod[1, s, :per_set]
             if k == 1:
-                own = own + prod[1, s, :per_set]
-            value = (own + rbuf[s, k].astype(F32) + bias).astype(BF16)
+                own = own + other
+            else:
+                first = first + other
+            earlier = jnp.where(tm == 0, first, rbuf[s, k].astype(F32))
+            value = (own + earlier + bias).astype(BF16)
             for q, i in enumerate(row_sets[s]):
                 out_ref[k, i] = value[q * cols : (q + 1) * cols]
 
@@ -303,7 +329,7 @@
                 pltpu.VMEM((3, 3, 3, channels, c_out), BF16),
                 pltpu.VMEM((frames, cols, channels), BF16),
                 pltpu.VMEM((frames, cols, channels), BF16),
-                pltpu.VMEM((n_tm * n_h, 2, channels), F32),
+                pltpu.VMEM((n_tm * n_h, 1, LANES), F32),
                 pltpu.VMEM((2, frames * per_set, 3 * channels), BF16),
                 pltpu.VMEM((3, 2, frames * per_set, c_out), F32),
                 pltpu.VMEM((2, 2, per_set, c_out), BF16),

time: 18.5 us -> 18 us (0.973)
  Pallas kernels: 17.6 us -> 17.1 us
    pallas_call x1, Pallas kernels: 17.6 us -> 17.1 us  [on_device(): pl.pallas_call(functools.partial(body, n_tm, n_h), out_shape=pltpu.VMEM((...]
where the time goes in v3:
time: 18 us; the launch traced here: 17.8 us
  Pallas kernels  17.1 us (95%)
  local copies, waits for them, and re-layouts  0.75 us (4%)
    pallas_call x1, Pallas kernels, on_device(): pl.pallas_call(functools.partial(body, n_tm, n_h), out_shape=pltpu.VMEM((...  17.1 us
    unnamed x1, local copies, waits for them, and re-layouts  0.75 us

profile of v3, /device:TPU:0, one launch (start us, length us, event | category | flops | bytes accessed | tf_op | source)
XLA Modules:
  0.0 17.8 jit_solution(12954122943239535648)
XLA Ops:
  0.0 17.1 %shard_map.55 = bf16[2,4,96,256]{3,2,1,0:T(8,128)(2,1)S(1)} custom-call(bf16[2,4,96,512]{3,2,1,0:T(8,128)(2,1)} %x_hbm.1, f32[1,512]{1,0:T(1,128)} %bitcast.3, f32[1,512]{1,0:T(1,128)} %bitcast.4, bf16[3,3,3,512,256]{4,3,2,1,0:T(8,128)(2,1)} %w_hbm.1, f32[1,256]{1,0:T(1,128)} %bitcast.5), custom_call_target="tpu_custom_call" | custom-call | tf_op jit(solution)/shard_map/pallas_call | solution.py:319
  17.1 0.7 %copy.7 = bf16[2,4,96,256]{3,2,1,0:T(8,128)(2,1)} copy(bf16[2,4,96,256]{3,2,1,0:T(8,128)(2,1)S(1)} %shard_map.55) | data formatting | bytes 786432

commit v4 on v3

--- a/solution.py
+++ b/solution.py
@@ -81,8 +81,9 @@
 
     for d in range(1, count):
         pl.semaphore_signal(barrier, inc=1, device_id=peer(d), device_id_type=MESH)
-    x_copy = pltpu.make_async_copy(x_hbm, x_vm, x_sem)
-    x_copy.start()
+    x_copies = [pltpu.make_async_copy(x_hbm.at[f], x_vm.at[f], x_sem.at[f]) for f in range(frames)]
+    for copy in x_copies:
+        copy.start()
     small = ((gain_hbm, gain_ref), (shift_hbm, shift_ref), (bias_hbm, bias_ref))
     p_copies = [pltpu.make_async_copy(*pair, p_sem.at[i]) for i, pair in enumerate(small)]
     for copy in p_copies:
@@ -91,13 +92,10 @@
         [pltpu.make_async_copy(w_hbm.at[a, :, c], w_vm.at[a, c], w_sem.at[a, c]) for c in range(3)]
         for a in range(3)
     ]
-    x_copy.wait()
-    for a in range(3):
-        for c in range(3):
-            w_copies[a][c].start()
     sums = jnp.zeros((8, channels), F32)
     squares = jnp.zeros((8, channels), F32)
     for f in range(frames):
+        x_copies[f].wait()
         for r in range(rows):
             v = x_vm[f, r].astype(F32).reshape(cols // 8, 8, channels)
             sums = sums + jnp.sum(v, axis=0)
@@ -128,6 +126,9 @@
     ]
     for copy in shares:
         copy.start()
+    for a in range(3):
+        for c in range(3):
+            w_copies[a][c].start()
     to_next = pltpu.make_async_remote_copy(
         src_ref=x_hbm.at[:, rows - 1],
         dst_ref=top_vm,
@@ -334,7 +335,7 @@
                 pltpu.VMEM((3, 2, frames * per_set, c_out), F32),
                 pltpu.VMEM((2, 2, per_set, c_out), BF16),
                 pltpu.VMEM((2, 2, per_set, c_out), BF16),
-                dma,
+                dma((frames,)),
                 dma((3,)),
                 dma((3, 3)),
                 dma((n_tm * n_h,)),

time: 18 us -> 18 us (level)
  no operation moved by 1% of the time
where the time goes in v4:
time: 18 us; the launch traced here: 17.8 us
  Pallas kernels  17.1 us (95%)
  local copies, waits for them, and re-layouts  0.75 us (4%)
    pallas_call x1, Pallas kernels, on_device(): pl.pallas_call(functools.partial(body, n_tm, n_h), out_shape=pltpu.VMEM((...  17.1 us
    unnamed x1, local copies, waits for them, and re-layouts  0.75 us

profile of v4, /device:TPU:0, one launch (start us, length us, event | category | flops | bytes accessed | tf_op | source)
XLA Modules:
  0.0 17.8 jit_solution(11448937439403478918)
XLA Ops:
  0.0 17.1 %shard_map.55 = bf16[2,4,96,256]{3,2,1,0:T(8,128)(2,1)S(1)} custom-call(bf16[2,4,96,512]{3,2,1,0:T(8,128)(2,1)} %x_hbm.1, f32[1,512]{1,0:T(1,128)} %bitcast.3, f32[1,512]{1,0:T(1,128)} %bitcast.4, bf16[3,3,3,512,256]{4,3,2,1,0:T(8,128)(2,1)} %w_hbm.1, f32[1,256]{1,0:T(1,128)} %bitcast.5), custom_call_target="tpu_custom_call" | custom-call | tf_op jit(solution)/shard_map/pallas_call | solution.py:320
  17.1 0.7 %copy.7 = bf16[2,4,96,256]{3,2,1,0:T(8,128)(2,1)} copy(bf16[2,4,96,256]{3,2,1,0:T(8,128)(2,1)S(1)} %shard_map.55) | data formatting | bytes 786432
